TPU v7x, 256 devices: a whole 4x4x8 slice. The times are simulated.
256 devices in a mesh: shuf: 64 (over y, z, core), rep: 4 (over x).
Axes of the slice: x: 4, y: 4, z: 8, core: 2. Of those that a mesh axis runs over, the one named last changes fastest.
Arguments:
- values: bfloat16 [524288, 1024], P('shuf', 'rep')
- subgroup: int32 [4096], P('shuf'), may hold values from 0 to 31
- owners: int32 [4096, 1], P('shuf'), may hold values from 0 to 63; in each aligned block of 64 rows (0 to 63, 64 to 127, ...) at most 2 rows name the same one
- col_gain: float32 [1024], P('rep'), may hold values from 0.5 to 1.5
- col_bias: float32 [1024], P('rep'), may hold values from -3 to 3
- out_weight: bfloat16 [1024, 1024], P('rep'), may hold values from -0.1875 to 0.1875
Outputs:
- projected: bfloat16 [524288, 1024], P(('shuf', 'rep'))
Inputs may be any that keep to these rules, and one draw needn't show every extreme that they name: `owners`: among the tiles of one index of shuf no owner is named more than 2 times, a bound that some block reaches.
All inputs are finite; a program needn't handle non-finite values.
Results may differ from a plain program's by a relative error of at most 0.015.
Values may be sent and summed in bfloat16 or wider, within the bound.
A program may use at most 64 MiB of HBM per device.

v0:
```python
import math

import jax
import jax.numpy as jnp
from jax import lax
from jax.sharding import PartitionSpec as P

GRP_DEV = 32
PRIOR = 256


def from_everyone(value, axis):
    peers = lax.axis_size(axis)
    return lax.all_to_all(
        jnp.broadcast_to(value[None], (peers, *value.shape)), axis, 0, 0, tiled=True
    )


def over_copies(value, axis):
    everything = from_everyone(value, axis)
    return jnp.sum(everything, axis=0)


def in_one(arrays, axis):
    flat, at, done = (jnp.concatenate([a.reshape(-1) for a in arrays]), 0, [])
    so_far = over_copies(flat, axis)
    for a in arrays:
        done.append(so_far[at : at + a.size].reshape(a.shape))
        at += a.size
    return tuple(done)


def side_by_side(arrays, axis, split_dim, concat_dim, along):
    widths = [math.prod(a.shape[along:]) for a in arrays]
    both = jnp.concatenate(
        [a.reshape(*a.shape[:along], w) for a, w in zip(arrays, widths)], axis=along
    )
    result = lax.all_to_all(both, axis, split_axis=split_dim, concat_axis=concat_dim, tiled=True)
    pieces = jnp.split(result, [sum(widths[:k]) for k in range(1, len(widths))], axis=along)
    return tuple(
        (b.reshape(*result.shape[:along], *a.shape[along:]) for a, b in zip(arrays, pieces))
    )


def in_one_piece(arrays, axis, split_dim, concat_dim, along):
    ends, at = ([], 0)
    for a in arrays[:-1]:
        at += a.shape[along]
        ends.append(at)
    both = jnp.concatenate(arrays, axis=along)
    return tuple(
        jnp.split(
            lax.all_to_all(both, axis, split_axis=split_dim, concat_axis=concat_dim, tiled=True),
            ends,
            axis=along,
        )
    )


def joined_along(pieces, dim):
    lengths = list(pieces.shape[1:])
    lengths[dim] *= pieces.shape[0]
    return jnp.moveaxis(pieces, 0, dim).reshape(lengths)


def gathered_copies(value, axis, dim):
    return joined_along(from_everyone(value, axis), dim)


def moments(group_sum, group_sq, count, mean_all, square_all):
    weight = (count + float(PRIOR))[:, None]
    center = (group_sum + float(PRIOR) * mean_all) / weight
    second = (group_sq + float(PRIOR) * square_all) / weight
    return (center, lax.rsqrt(second - center * center + 1e-05))


def slot_places(target, capacity, peer_count):
    one_hot = (target[:, None] == jnp.arange(peer_count, dtype=jnp.int32)[None, :]).astype(
        jnp.int32
    )
    position = jnp.sum((jnp.cumsum(one_hot, axis=0) - one_hot) * one_hot, axis=1)
    return target * capacity + position


def on_device(values, subgroup, owners, col_gain, col_bias, out_weight):
    local_rows, local_cols = values.shape
    tile_count = subgroup.shape[0]
    tile_rows = local_rows // tile_count
    peer_count = lax.axis_size("shuf")
    shaped = values.reshape(tile_count, tile_rows, local_cols)
    widened = shaped.astype(jnp.float32)
    tile_sum = jnp.sum(widened, axis=1)
    tile_sq = jnp.sum(widened * widened, axis=1)
    col_sum, col_square = in_one((jnp.sum(tile_sum, axis=0), jnp.sum(tile_sq, axis=0)), "shuf")
    row_count = float(local_rows * peer_count)
    mean_all = col_sum / row_count
    square_all = col_square / row_count
    target = owners[:, 0]
    capacity = max(2, 2 * tile_count // peer_count)
    slot_index = slot_places(target, capacity, peer_count)
    packed = jnp.concatenate([tile_sum, tile_sq], axis=1)
    outgoing = (
        jnp.zeros((peer_count * capacity, 2 * local_cols), jnp.float32).at[slot_index].set(packed)
    )
    labels = (
        jnp.full((peer_count * capacity,), -1.0, jnp.float32)
        .at[slot_index]
        .set(subgroup.astype(jnp.float32))
    )
    arrived, arrived_labels = tuple(
        (
            part.astype(jnp.float32)
            for part in side_by_side(
                (outgoing.astype(jnp.bfloat16), labels.astype(jnp.bfloat16)), "shuf", 0, 0, 1
            )
        )
    )
    group_ids = arrived_labels.astype(jnp.int32)
    members = (group_ids[:, None] == jnp.arange(GRP_DEV, dtype=jnp.int32)[None, :]).astype(
        jnp.float32
    )
    group_sum = jnp.dot(members.T, arrived[:, :local_cols])
    group_sq = jnp.dot(members.T, arrived[:, local_cols:])
    count = float(tile_rows) * jnp.sum(members, axis=0)
    center, inverse = moments(group_sum, group_sq, count, mean_all, square_all)
    slot_center = jnp.dot(members, center)
    slot_inverse = jnp.dot(members, inverse)
    back_center, back_inverse = tuple(
        (
            part.astype(jnp.float32)
            for part in in_one_piece(
                (slot_center.astype(jnp.bfloat16), slot_inverse.astype(jnp.bfloat16)),
                "shuf",
                0,
                0,
                1,
            )
        )
    )
    tile_center = back_center[slot_index]
    tile_scale = back_inverse[slot_index] * col_gain
    scored = ((widened - tile_center[:, None, :]) * tile_scale[:, None, :] + col_bias).astype(
        jnp.bfloat16
    )
    standard = scored.reshape(local_rows, local_cols)
    full_rows = lax.all_to_all(standard, "rep", split_axis=0, concat_axis=1, tiled=True)
    full_weight = gathered_copies(out_weight, "rep", 0)
    summed = jnp.zeros((full_rows.shape[0], full_weight.shape[1]), jnp.float32)
    for block in range(lax.axis_size("rep")):
        partial_value = jnp.dot(
            full_rows[:, block * local_cols : (block + 1) * local_cols],
            full_weight[block * local_cols : (block + 1) * local_cols],
            preferred_element_type=jnp.float32,
        )
        summed = summed + partial_value.astype(jnp.bfloat16).astype(jnp.float32)
    return summed.astype(jnp.bfloat16)


def solution(mesh):
    return jax.shard_map(
        on_device,
        mesh=mesh,
        in_specs=(P("shuf", "rep"), P("shuf"), P("shuf", None), P("rep"), P("rep"), P("rep", None)),
        out_specs=P(("shuf", "rep"), None),
        check_vma=False,
    )
```

profile of v0, /device:TPU:1, one launch (start us, length us, event | category | flops | bytes accessed | tf_op | source)
XLA Modules:
  0.0 159.9 jit_solution(14804359981047646363)
XLA Ops:
  0.0 3.3 %convert_reduce_fusion = (f32[256]{0:T(256)S(1)}, f32[256]{0:T(256)S(1)}) fusion(bf16[8192,256]{1,0:T(8,128)(2,1)} %param.6), kind=kLoop, calls=%fused_computation.11 | loop fusion | flops 8388096 | bytes 4196352 | tf_op jit(solution)/shard_map/reduce_sum | solution.py:94
  3.4 0.7 broadcast_in_dim.10
  4.1 13.1 %all-to-all-start.1 = ((f32[64,1,512]{2,1,0:T(1,128)}), f32[64,1,512]{2,1,0:T(1,128)S(1)}, u32[]{:S(2)}, u32[]{:S(2)}) async-start(f32[64,1,512]{2,1,0:T(1,128)} %broadcast_in_dim.10), calls=%async_computation.1 | async-start | bytes 262144 | tf_op jit(solution)/shard_map/all_to_all | solution.py:14
  17.2 4.6 %bitcast_reduce_fusion = (f32[64,256]{1,0:T(8,128)S(1)}, f32[64,256]{1,0:T(8,128)S(1)}) fusion(bf16[8192,256]{1,0:T(8,128)(2,1)} %param.6), kind=kLoop, calls=%fused_computation.9 | loop fusion | flops 8355840 | bytes 4325376 | tf_op jit(solution)/shard_map/reduce_sum | solution.py:92
  22.1 0.2 select_reduce_fusion
  22.3 0.8 scatter_custom_fusion.1
  23.1 0.2 concatenate.23
  23.3 0.9 scatter_custom_fusion
  24.3 0.8 pad_maximum_fusion
  25.1 2.4 %all-to-all-done.1 = f32[64,1,512]{2,1,0:T(1,128)S(1)} async-done(((f32[64,1,512]{2,1,0:T(1,128)}), f32[64,1,512]{2,1,0:T(1,128)S(1)}, u32[]{:S(2)}, u32[]{:S(2)}) %all-to-all-start.1) | async-done | bytes 131104 | tf_op jit(solution)/shard_map/all_to_all | solution.py:14
  27.5 7.9 %all-to-all-start = ((bf16[64,2,513]{2,1,0:T(2,128)(2,1)}), bf16[64,2,513]{2,1,0:T(2,128)(2,1)S(1)}, u32[]{:S(2)}, u32[]{:S(2)}) async-start(bf16[64,2,513]{2,1,0:T(2,128)(2,1)} %pad_maximum_fusion), calls=%async_computation | async-start | bytes 327680 | tf_op jit(solution)/shard_map/all_to_all | solution.py:38
  35.5 0.1 reduce_sum.71
  35.6 10.5 %all-to-all-done = bf16[64,2,513]{2,1,0:T(2,128)(2,1)S(1)} async-done(((bf16[64,2,513]{2,1,0:T(2,128)(2,1)}), bf16[64,2,513]{2,1,0:T(2,128)(2,1)S(1)}, u32[]{:S(2)}, u32[]{:S(2)}) %all-to-all-start) | async-done | bytes 131360 | tf_op jit(solution)/shard_map/all_to_all | solution.py:38
  46.1 0.1 all_to_all.36
  46.4 0.1 fusion.8
  46.6 0.2 convolution_convert_fusion.1
  46.8 0.3 convolution_convert_fusion
  47.1 0.7 all_to_all.38
  47.8 5.3 %all-to-all-start.2 = ((bf16[64,2,512]{2,1,0:T(2,128)(2,1)}), bf16[64,2,512]{2,1,0:T(2,128)(2,1)S(1)}, u32[]{:S(2)}, u32[]{:S(2)}) async-start(bf16[64,2,512]{2,1,0:T(2,128)(2,1)} %all_to_all.38), calls=%async_computation.2 | async-start | bytes 262144 | tf_op jit(solution)/shard_map/all_to_all | solution.py:53
  53.2 10.3 %all-to-all-done.2 = bf16[64,2,512]{2,1,0:T(2,128)(2,1)S(1)} async-done(((bf16[64,2,512]{2,1,0:T(2,128)(2,1)}), bf16[64,2,512]{2,1,0:T(2,128)(2,1)S(1)}, u32[]{:S(2)}, u32[]{:S(2)}) %all-to-all-start.2) | async-done | bytes 131104 | tf_op jit(solution)/shard_map/all_to_all | solution.py:53
  63.6 0.7 gather_fusion
  64.2 0.7 gather_fusion.1
  64.9 3.6 %fusion.1 = bf16[8192,256]{1,0:T(8,128)(2,1)S(1)} fusion(bf16[8192,256]{1,0:T(8,128)(2,1)} %param.6, f32[256]{0:T(256)S(1)} %copy-done.4, f32[64,256]{1,0:T(8,128)S(1)} %broadcast_multiply_fusion, f32[64,256]{1,0:T(8,128)S(1)} %gather_fusion), kind=kLoop, calls=%fused_computation.6 | loop fusion | flops 10485760 | bytes 8520704 | tf_op jit(solution)/shard_map/convert_element_type | solution.py:142
  68.5 52.0 %all_to_all.51 = bf16[4,2048,256]{2,1,0:T(8,128)(2,1)} all-to-all(bf16[4,2048,256]{2,1,0:T(8,128)(2,1)S(1)} %bitcast.45), channel_id=1, replica_groups=mesh['shuf'=64,'rep'=4] {'rep'}, dimensions={0} | all-to-all | bytes 8388608 | tf_op jit(solution)/shard_map/all_to_all | solution.py:146
  120.5 1.6 %broadcast_in_dim.11 = bf16[4,256,1024]{2,1,0:T(8,128)(2,1)} broadcast(bf16[256,1024]{1,0:T(8,128)(2,1)S(1)} %copy-done.1), dimensions={1,2} | broadcast | bytes 2621440 | tf_op jit(solution)/shard_map/broadcast_in_dim | solution.py:15
  122.1 3.8 %all-to-all-start.4 = ((bf16[4,256,1024]{2,1,0:T(8,128)(2,1)}), bf16[4,256,1024]{2,1,0:T(8,128)(2,1)S(1)}, u32[]{:S(2)}, u32[]{:S(2)}) async-start(bf16[4,256,1024]{2,1,0:T(8,128)(2,1)} %broadcast_in_dim.11), calls=%async_computation.4 | async-start | bytes 4194304 | tf_op jit(solution)/shard_map/all_to_all | solution.py:14
  125.9 6.2 %copy.14 = bf16[2048,4,256]{0,2,1:T(8,128)(2,1)} copy(bf16[2048,4,256]{2,0,1:T(8,128)(2,1)} %bitcast.44) | data formatting | bytes 8388608 | tf_op jit(solution)/shard_map/all_to_all | solution.py:146
  132.1 18.2 %all-to-all-done.4 = bf16[4,256,1024]{2,1,0:T(8,128)(2,1)S(1)} async-done(((bf16[4,256,1024]{2,1,0:T(8,128)(2,1)}), bf16[4,256,1024]{2,1,0:T(8,128)(2,1)S(1)}, u32[]{:S(2)}, u32[]{:S(2)}) %all-to-all-start.4) | async-done | bytes 2097184 | tf_op jit(solution)/shard_map/all_to_all | solution.py:14
  150.3 2.7 %fusion.10 = bf16[2048,1024]{1,0:T(8,128)(2,1)S(1)} fusion(bf16[2048,1024]{0,1:T(8,128)(2,1)} %bitcast.40, bf16[4,256,1024]{2,1,0:T(8,128)(2,1)S(1)} %all-to-all-done.4), kind=kOutput, calls=%fused_computation.25 | convolution fusion | flops 1073741824 | bytes 5767168 | tf_op jit(solution)/shard_map/dot_general | solution.py:150
  153.0 1.3 fusion.12
  154.3 1.3 fusion.14
  155.6 4.3 %add_convert_fusion = bf16[2048,1024]{1,0:T(8,128)(2,1)} fusion(bf16[2048,1024]{1,0:T(8,128)(2,1)S(1)} %fusion.10, bf16[2048,1024]{1,0:T(8,128)(2,1)S(1)} %fusion.12, bf16[2048,1024]{1,0:T(8,128)(2,1)S(1)} %fusion.14, bf16[2048,1024]{0,1:T(8,128)(2,1)S(1)} %bitcast.43, bf16[4,256,1024]{2,1,0:T(8,128)(2,1)S(1)} %all-to-all-done.4), kind=kOutput, calls=%fused_computation.14 | convolution fusion | flops 1092616192 | bytes 18350080 | tf_op jit(solution)/shard_map/dot_general | solution.py:150
  (29 shorter events, 0.6 us)
Async XLA Ops:
  0.0 21.9 %copy-start.5 = (s32[64]{0:T(128)S(1)}, s32[64]{0:T(128)}, u32[]{:S(2)}) copy-start(s32[64]{0:T(128)} %param.7) | copy-start | bytes 772
  0.0 21.9 %copy-start.2 = (s32[64,1]{0,1:T(1,128)S(1)}, s32[64,1]{0,1:T(1,128)}, u32[]{:S(2)}) copy-start(s32[64,1]{0,1:T(1,128)} %param.8) | copy-start | bytes 772
  4.1 23.5 %all-to-all-start.1 = ((f32[64,1,512]{2,1,0:T(1,128)}), f32[64,1,512]{2,1,0:T(1,128)S(1)}, u32[]{:S(2)}, u32[]{:S(2)}) async-start(f32[64,1,512]{2,1,0:T(1,128)} %broadcast_in_dim.10), calls=%async_computation.1 | async-start | bytes 262144 | tf_op jit(solution)/shard_map/all_to_all | solution.py:14
  17.2 47.7 %copy-start.3 = (f32[256]{0:T(256)S(1)}, f32[256]{0:T(256)}, u32[]{:S(2)}) copy-start(f32[256]{0:T(256)} %param.9) | copy-start | bytes 3076
  17.2 47.7 %copy-start.4 = (f32[256]{0:T(256)S(1)}, f32[256]{0:T(256)}, u32[]{:S(2)}) copy-start(f32[256]{0:T(256)} %param.10) | copy-start | bytes 3076
  27.5 18.5 %all-to-all-start = ((bf16[64,2,513]{2,1,0:T(2,128)(2,1)}), bf16[64,2,513]{2,1,0:T(2,128)(2,1)S(1)}, u32[]{:S(2)}, u32[]{:S(2)}) async-start(bf16[64,2,513]{2,1,0:T(2,128)(2,1)} %pad_maximum_fusion), calls=%async_computation | async-start | bytes 327680 | tf_op jit(solution)/shard_map/all_to_all | solution.py:38
  47.8 15.7 %all-to-all-start.2 = ((bf16[64,2,512]{2,1,0:T(2,128)(2,1)}), bf16[64,2,512]{2,1,0:T(2,128)(2,1)S(1)}, u32[]{:S(2)}, u32[]{:S(2)}) async-start(bf16[64,2,512]{2,1,0:T(2,128)(2,1)} %all_to_all.38), calls=%async_computation.2 | async-start | bytes 262144 | tf_op jit(solution)/shard_map/all_to_all | solution.py:53
  68.5 52.0 %copy-start.1 = (bf16[256,1024]{1,0:T(8,128)(2,1)S(1)}, bf16[256,1024]{1,0:T(8,128)(2,1)}, u32[]{:S(2)}) copy-start(bf16[256,1024]{1,0:T(8,128)(2,1)} %param.11) | copy-start | bytes 1572868
  122.1 28.2 %all-to-all-start.4 = ((bf16[4,256,1024]{2,1,0:T(8,128)(2,1)}), bf16[4,256,1024]{2,1,0:T(8,128)(2,1)S(1)}, u32[]{:S(2)}, u32[]{:S(2)}) async-start(bf16[4,256,1024]{2,1,0:T(8,128)(2,1)} %broadcast_in_dim.11), calls=%async_computation.4 | async-start | bytes 4194304 | tf_op jit(solution)/shard_map/all_to_all | solution.py:14
  150.3 2.7 %copy-start = (bf16[2048,4,256]{0,2,1:T(8,128)(2,1)S(1)}, bf16[2048,4,256]{0,2,1:T(8,128)(2,1)}, u32[]{:S(2)}) copy-start(bf16[2048,4,256]{0,2,1:T(8,128)(2,1)} %copy.14) | copy-start | bytes 12582916
where the time goes:
time: 161 us; the launch traced here: 160 us
  blocking collectives  52 us (32%)
  waiting for transfers between devices  41.4 us (26%)
  starting transfers between devices  30.1 us (19%)
  other arithmetic  14 us (9%)
  local copies, waits for them, and re-layouts  11.8 us (7%)
  matrix products  10.2 us (6%)
    all_to_all x1, blocking collectives, on_device(): lax.all_to_all(standard, 'rep', split_axis=0, concat_axis=1, tiled=True)  52 us
    all_to_all x2, waiting for transfers between devices, from_everyone(): lax.all_to_all(jnp.broadcast_to(value[None], (peers, *value.shape)), axis...  20.6 us
    all_to_all x2, starting transfers between devices, from_everyone(): lax.all_to_all(jnp.broadcast_to(value[None], (peers, *value.shape)), axis...  16.9 us
    all_to_all x1, waiting for transfers between devices, side_by_side(): lax.all_to_all(both, axis, split_axis=split_dim, concat_axis=concat_dim,...  10.5 us
    all_to_all x1, waiting for transfers between devices, in_one_piece(): lax.all_to_all(both, axis, split_axis=split_dim, concat_axis=concat_dim,...  10.3 us
    dot_general x4, matrix products, on_device(): jnp.dot(full_rows[:, block * local_cols:(block + 1) * local_cols], full_w...  9.55 us
    all_to_all x1, starting transfers between devices, side_by_side(): lax.all_to_all(both, axis, split_axis=split_dim, concat_axis=concat_dim,...  7.9 us
    all_to_all x1, local copies, waits for them, and re-layouts, on_device(): lax.all_to_all(standard, 'rep', split_axis=0, concat_axis=1, tiled=True)  6.2 us
  transfers between devices with their start and end apart: 4, of which 4 were waited for; matrix products, arithmetic and copies ran while one was open for 9% of the time, Pallas kernels for 0%

commit v1 on v0

v1 whole, which is shorter than its diff:
```python
import jax
import jax.numpy as jnp
from jax import lax
from jax.experimental import pallas as pl
from jax.experimental.pallas import tpu as pltpu
from jax.sharding import PartitionSpec as P

TILE = 128
TILES = 64
GRP_DEV = 32
PRIOR = 256.0
COLS = 256
OUT = 1024
ROWS = 8192
OROWS = 2048
NX, NY, NZ, NC = 4, 4, 8, 2
NQ = NY * NC
SLOTS = 2 * NQ * NZ
GRPS = 8
GROWS = OROWS // GRPS
EARLY = 6
MSG = 2 * COLS + 128
MESH = pl.DeviceIdType.MESH
F32, BF16 = jnp.float32, jnp.bfloat16


def shuf_index(y, z, c):
    return (y * NZ + z) * NC + c


def iota(shape, dim):
    return lax.broadcasted_iota(jnp.int32, shape, dim)


def pick(matrix, rows):
    return jnp.dot(matrix, rows, preferred_element_type=F32)


def exchange(
    values, subgroup, owners, gain, bias, weight,
    out,
    vals, raw, wall, subs, owns, gb, tstat, totals, tot_y, tot_z,
    send_y, buf_y, send_z, buf_z, back_z, got_z, back_y, got_y, tile_stat, peer_stat, par, lhs,
    load_sem, aux_sem, x_send, x_recv, wx_send, wx_recv, wz_send, wz_recv, wy_send, wy_recv,
    wc_send, wc_recv, gb_send, gb_recv, st_send, st_recv, line_send, line_recv, near, far,
):
    shuf, x = lax.axis_index("shuf"), lax.axis_index("rep")
    y, z, c = shuf // (NZ * NC), lax.rem(shuf // NC, NZ), lax.rem(shuf, NC)
    q = y * NC + c
    barrier = pltpu.get_barrier_semaphore()

    def x_peer(d):
        return (shuf, lax.rem(x + d, NX))

    def z_peer(d):
        return (shuf_index(y, lax.rem(z + d, NZ), c), x)

    def q_peer(d):
        p = lax.rem(q + d, NQ)
        return (shuf_index(p // NC, z, lax.rem(p, NC)), x)

    def signal(sem, to):
        pl.semaphore_signal(sem, inc=1, device_id=to, device_id_type=MESH)

    def send(src, dst, s, r, to):
        pltpu.make_async_remote_copy(src, dst, s, r, device_id=to, device_id_type=MESH).start()

    def wait_for(ref, sem):
        pltpu.make_async_copy(ref, ref, sem).wait()

    @pl.when(x == 0)
    def _():
        for d in range(1, NX):
            signal(barrier, x_peer(d))

    @pl.when(x != 0)
    def _():
        for d in range(1, NX):
            @pl.when(x + d != NX)
            def _():
                signal(barrier, x_peer(d))
        pl.semaphore_wait(barrier, NX - 1)
        signal(near, (shuf, 0))

    @pl.when(x == 0)
    def _():
        pl.semaphore_wait(near, NX - 1)

    w_rows = pl.ds(pl.multiple_of((c * NZ + z) * 16, 16), 16)
    w_cols = pl.ds(pl.multiple_of(y * 256, 256), 256)
    for d in range(1, NX):
        at = NX - d
        send(
            weight.at[w_rows, w_cols],
            wall.at[pl.ds(pl.multiple_of(at * COLS + (c * NZ + z) * 16, 16), 16), w_cols],
            wx_send, wx_recv, x_peer(d),
        )
        send(gain, gb.at[at, 0], gb_send, gb_recv, x_peer(d))
        send(bias, gb.at[at, 1], gb_send, gb_recv, x_peer(d))

    def send_group(g):
        for d in (2, 1, 3):
            first = lax.rem(x + d, NX) * OROWS + g * GROWS
            send(
                values.at[pl.ds(pl.multiple_of(first, GROWS), GROWS)],
                raw.at[NX - d - 1, pl.ds(g * GROWS, GROWS)],
                x_send, x_recv.at[NX - d - 1, g], x_peer(d),
            )

    for g in range(EARLY):
        send_group(g)

    @pl.when(x == 0)
    def _():
        for d in range(1, NQ):
            signal(barrier, q_peer(d))
        for d in range(1, NZ):
            signal(barrier, z_peer(d))

    loads = []
    for i in range(8):
        part = pl.ds(i * 1024, 1024)
        loads.append(pltpu.make_async_copy(values.at[part], vals.at[part], load_sem.at[i]))
        loads[-1].start()
    aux = [
        pltpu.make_async_copy(subgroup, subs, aux_sem.at[0]),
        pltpu.make_async_copy(owners, owns, aux_sem.at[1]),
        pltpu.make_async_copy(weight, wall.at[pl.ds(0, COLS)], aux_sem.at[2]),
        pltpu.make_async_copy(gain, gb.at[0, 0], aux_sem.at[3]),
        pltpu.make_async_copy(bias, gb.at[0, 1], aux_sem.at[4]),
    ]
    for a in aux:
        a.start()

    @pl.loop(0, 8)
    def _(i):
        wait_for(vals.at[pl.ds(0, 1024)], load_sem.at[i])

        @pl.loop(0, 8)
        def _(j):
            t = i * 8 + j
            a = jnp.zeros((8, COLS), F32)
            b = jnp.zeros((8, COLS), F32)
            for k in range(TILE // 16):
                v = vals[pl.ds(pl.multiple_of(t * TILE + k * 16, 16), 16), :].astype(F32)
                lo, hi = v[:8], v[8:]
                a = a + lo + hi
                b = b + lo * lo + hi * hi
            tstat[pl.ds(t, 1), :COLS] = jnp.sum(a, axis=0, keepdims=True)
            tstat[pl.ds(t, 1), COLS:] = jnp.sum(b, axis=0, keepdims=True)

    sums = tstat[...]
    own_total = jnp.sum(sums, axis=0, keepdims=True)
    totals[0] = own_total
    tot_y[q] = own_total

    for a in aux[:2]:
        a.wait()
    lane = iota((8, TILES), 1)
    own_row = jnp.zeros((8, TILES), jnp.int32)
    sub_row = jnp.zeros((8, TILES), jnp.int32)
    for t in range(TILES):
        own_row = jnp.where(lane == t, owns[t], own_row)
        sub_row = jnp.where(lane == t, subs[t], sub_row)
    i0, i1 = iota((TILES, TILES), 0), iota((TILES, TILES), 1)
    eye = i0 == i1

    def as_rows(row):
        return jnp.broadcast_to(row[:1], (TILES, TILES))

    def as_column(row):
        spread = jnp.where(eye, as_rows(row), 0).astype(F32)
        return jnp.sum(spread, axis=1, keepdims=True).astype(jnp.int32)

    same = (as_rows(own_row) == as_column(own_row)) & (i0 < i1)
    pos = jnp.sum(jnp.where(same, 1.0, 0.0), axis=0, keepdims=True).astype(jnp.int32)
    o = own_row[:1]
    slot = ((((o >> 4) * NC + (o & 1)) * NZ + ((o >> 1) & 7)) * 2) + pos
    slot_col = as_column(slot)
    to_slot = jnp.where(iota((SLOTS, TILES), 0) == slot, 1.0, 0.0).astype(BF16)
    from_slot = jnp.where(iota((TILES, SLOTS), 1) == slot_col, 1.0, 0.0).astype(BF16)
    label = jnp.where(iota((TILES, 128), 1) == as_column(sub_row), 1.0, 0.0).astype(BF16)
    packed = jnp.concatenate([sums.astype(BF16), label], axis=1)
    send_y[...] = pick(to_slot, packed).astype(BF16).reshape(NQ, 16, MSG)
    buf_y[q] = send_y[q]

    r0, r1 = iota((SLOTS, SLOTS), 0), iota((SLOTS, SLOTS), 1)
    swap = jnp.where(r1 == ((r0 >> 1) & 7) * 16 + (r0 >> 4) * 2 + (r0 & 1), 1.0, 0.0).astype(BF16)

    @pl.when(x == 0)
    def _():
        pl.semaphore_wait(barrier, NQ - 1 + NZ - 1)
        for d in range(1, NX):
            signal(far, x_peer(d))

    @pl.when(x != 0)
    def _():
        pl.semaphore_wait(far, 1)

    for d in range(1, NQ):
        p = lax.rem(q + d, NQ)
        send(totals.at[0], tot_y.at[q], line_send.at[0], line_recv.at[0], q_peer(d))
        send(send_y.at[p], buf_y.at[q], line_send.at[1], line_recv.at[1], q_peer(d))

    wait_for(wall.at[pl.ds(0, 48), pl.ds(0, 256)], wx_recv)
    for d in range(1, NZ):
        for b in range(1, NX):
            piece = wall.at[pl.ds(pl.multiple_of(b * COLS + (c * NZ + z) * 16, 16), 16), w_cols]
            send(piece, piece, wz_send, wz_recv, z_peer(d))

    wait_for(tot_y.at[pl.ds(0, NQ - 1)], line_recv.at[0])
    wait_for(buf_y.at[pl.ds(0, NQ - 1)], line_recv.at[1])
    line_total = jnp.sum(tot_y[...], axis=0)
    totals[1] = line_total
    tot_z[z] = line_total
    send_z[...] = pick(swap, buf_y[...].reshape(SLOTS, MSG)).astype(BF16).reshape(NZ, 16, MSG)
    buf_z[z] = send_z[z]
    for d in range(1, NZ):
        p = lax.rem(z + d, NZ)
        send(totals.at[1], tot_z.at[z], line_send.at[2], line_recv.at[2], z_peer(d))
        send(send_z.at[p], buf_z.at[z], line_send.at[3], line_recv.at[3], z_peer(d))

    wait_for(wall.at[pl.ds(0, (NX - 1) * (NZ - 1) * 16), pl.ds(0, 256)], wz_recv)
    for d in range(1, NY):
        for b in range(1, NX):
            piece = wall.at[pl.ds(pl.multiple_of(b * COLS + c * 128, 128), 128), w_cols]
            send(piece, piece, wy_send, wy_recv, q_peer(NC * d))

    wait_for(tot_z.at[pl.ds(0, NZ - 1)], line_recv.at[2])
    wait_for(buf_z.at[pl.ds(0, NZ - 1)], line_recv.at[3])
    total = jnp.sum(tot_z[...], axis=0) / float(ROWS * NQ * NZ)
    arrived = buf_z[...].reshape(SLOTS, MSG)
    member = arrived[:, 2 * COLS:]
    member_t = jnp.transpose(member.astype(F32))[:GRP_DEV].astype(BF16)
    group = pick(member_t, arrived[:, : 2 * COLS])
    count = float(TILE) * jnp.sum(member_t.astype(F32), axis=1, keepdims=True)
    blended = (group + PRIOR * total) / (count + PRIOR)
    center, second = blended[:, :COLS], blended[:, COLS:]
    inverse = lax.rsqrt(second - center * center + 1e-05)
    both = jnp.concatenate([center, inverse], axis=1).astype(BF16)
    both = jnp.concatenate([both, jnp.zeros((128 - GRP_DEV, 2 * COLS), BF16)], axis=0)
    back_z[...] = pick(member, both).astype(BF16).reshape(NZ, 16, 2 * COLS)
    got_z[z] = back_z[z]
    for d in range(1, NZ):
        p = lax.rem(z + d, NZ)
        send(back_z.at[p], got_z.at[z], line_send.at[4], line_recv.at[4], z_peer(d))

    wait_for(got_z.at[pl.ds(0, NZ - 1)], line_recv.at[4])
    back_y[...] = pick(swap, got_z[...].reshape(SLOTS, 2 * COLS)).astype(BF16).reshape(NQ, 16, 2 * COLS)
    got_y[q] = back_y[q]
    for d in range(1, NQ):
        p = lax.rem(q + d, NQ)
        send(back_y.at[p], got_y.at[q], line_send.at[5], line_recv.at[5], q_peer(d))

    wait_for(wall.at[pl.ds(0, 3 * 128), pl.ds(0, 768)], wy_recv)
    for b in range(1, NX):
        piece = wall.at[pl.ds(pl.multiple_of(b * COLS + c * 128, 128), 128)]
        send(piece, piece, wc_send, wc_recv, (shuf_index(y, z, 1 - c), x))

    wait_for(got_y.at[pl.ds(0, NQ - 1)], line_recv.at[5])
    tile_stat[...] = pick(from_slot, got_y[...].reshape(SLOTS, 2 * COLS)).astype(BF16)
    for d in range(1, NX):
        rows = pl.ds(pl.multiple_of(lax.rem(x + d, NX) * 16, 16), 16)
        send(tile_stat.at[rows], peer_stat.at[NX - d - 1], st_send, st_recv, x_peer(d))
    for g in range(EARLY, GRPS):
        send_group(g)

    for a in aux[2:]:
        a.wait()
    wait_for(gb.at[pl.ds(0, NX - 1)], gb_recv)
    wait_for(wall.at[pl.ds(0, 3 * 128)], wc_recv)
    own_rows = pl.ds(pl.multiple_of(x * 16, 16), 16)
    stats = [tile_stat[own_rows, :]]
    wait_for(peer_stat, st_recv)
    stats += [peer_stat[d] for d in range(NX - 1)]
    for d in range(NX):
        s = stats[d].astype(F32)
        par[0, :, d * COLS:(d + 1) * COLS] = s[:, :COLS]
        par[1, :, d * COLS:(d + 1) * COLS] = s[:, COLS:] * gb[d, 0:1, :]

    @pl.loop(0, GRPS)
    def _(g):
        for d in range(1, NX):
            wait_for(raw.at[d - 1, pl.ds(0, GROWS)], x_recv.at[d - 1, g])
        for j in range(GROWS // TILE):
            t = g * (GROWS // TILE) + j
            for d in range(NX):
                cols = slice(d * COLS, (d + 1) * COLS)
                if d == 0:
                    first = x * OROWS + t * TILE
                    v = vals[pl.ds(pl.multiple_of(first, TILE), TILE), :]
                else:
                    v = raw[d - 1, pl.ds(pl.multiple_of(t * TILE, TILE), TILE), :]
                scored = (v.astype(F32) - par[0, pl.ds(t, 1), cols]) * par[1, pl.ds(t, 1), cols]
                lhs[j * TILE:(j + 1) * TILE, cols] = (scored + gb[d, 1:2, :]).astype(BF16)
        rows = pl.ds(pl.multiple_of(g * GROWS, GROWS), GROWS)
        out[rows, :] = jnp.dot(lhs[...], wall[...], preferred_element_type=F32).astype(BF16)

    wait_for(raw, x_send)
    wait_for(wall.at[pl.ds(0, 48), pl.ds(0, 256)], wx_send)
    wait_for(wall.at[pl.ds(0, (NX - 1) * (NZ - 1) * 16), pl.ds(0, 256)], wz_send)
    wait_for(wall.at[pl.ds(0, 3 * 128), pl.ds(0, 768)], wy_send)
    wait_for(wall.at[pl.ds(0, 3 * 128)], wc_send)
    wait_for(gb.at[pl.ds(0, NX - 1)], gb_send)
    wait_for(peer_stat, st_send)
    wait_for(tot_y.at[pl.ds(0, NQ - 1)], line_send.at[0])
    wait_for(buf_y.at[pl.ds(0, NQ - 1)], line_send.at[1])
    wait_for(tot_z.at[pl.ds(0, NZ - 1)], line_send.at[2])
    wait_for(buf_z.at[pl.ds(0, NZ - 1)], line_send.at[3])
    wait_for(got_z.at[pl.ds(0, NZ - 1)], line_send.at[4])
    wait_for(got_y.at[pl.ds(0, NQ - 1)], line_send.at[5])


def write_out(src, dst, sem):
    copies = []
    for i in range(4):
        rows = pl.ds(i * (OROWS // 4), OROWS // 4)
        copies.append(pltpu.make_async_copy(src.at[rows], dst.at[rows], sem.at[i]))
        copies[-1].start()
    for copy in copies:
        copy.wait()


def on_device(values, subgroup, owners, col_gain, col_bias, out_weight):
    dma, vmem = pltpu.SemaphoreType.DMA, pltpu.VMEM
    hbm = pl.BlockSpec(memory_space=pltpu.HBM)
    rows = pl.pallas_call(
        exchange,
        out_shape=pltpu.VMEM((OROWS, OUT), BF16),
        in_specs=[hbm] * 6,
        out_specs=pl.BlockSpec(memory_space=pltpu.VMEM),
        scratch_shapes=[
            vmem((ROWS, COLS), BF16),
            vmem((NX - 1, OROWS, COLS), BF16),
            vmem((NX * COLS, OUT), BF16),
            pltpu.SMEM((TILES,), jnp.int32),
            pltpu.SMEM((TILES,), jnp.int32),
            vmem((NX, 2, COLS), F32),
            vmem((TILES, 2 * COLS), F32),
            vmem((2, 1, 2 * COLS), F32),
            vmem((NQ, 1, 2 * COLS), F32),
            vmem((NZ, 1, 2 * COLS), F32),
            vmem((NQ, 16, MSG), BF16),
            vmem((NQ, 16, MSG), BF16),
            vmem((NZ, 16, MSG), BF16),
            vmem((NZ, 16, MSG), BF16),
            vmem((NZ, 16, 2 * COLS), BF16),
            vmem((NZ, 16, 2 * COLS), BF16),
            vmem((NQ, 16, 2 * COLS), BF16),
            vmem((NQ, 16, 2 * COLS), BF16),
            vmem((TILES, 2 * COLS), BF16),
            vmem((NX - 1, 16, 2 * COLS), BF16),
            vmem((2, 16, NX * COLS), F32),
            vmem((GROWS, NX * COLS), BF16),
            dma((8,)), dma((5,)), dma, dma((NX - 1, GRPS)),
            dma, dma, dma, dma, dma, dma, dma, dma, dma, dma, dma, dma,
            dma((6,)), dma((6,)),
            pltpu.SemaphoreType.REGULAR, pltpu.SemaphoreType.REGULAR,
        ],
        compiler_params=pltpu.CompilerParams(
            collective_id=0, has_side_effects=True, vmem_limit_bytes=32 * 1024 * 1024
        ),
    )(values, subgroup, owners.reshape(TILES), col_gain, col_bias, out_weight)
    return pl.pallas_call(
        write_out,
        out_shape=jax.ShapeDtypeStruct((OROWS, OUT), BF16),
        in_specs=[pl.BlockSpec(memory_space=pltpu.VMEM)],
        out_specs=pl.BlockSpec(memory_space=pltpu.HBM),
        scratch_shapes=[dma((4,))],
        compiler_params=pltpu.CompilerParams(vmem_limit_bytes=1024 * 1024),
    )(rows)


def solution(mesh):
    return jax.shard_map(
        on_device,
        mesh=mesh,
        in_specs=(P("shuf", "rep"), P("shuf"), P("shuf", None), P("rep"), P("rep"), P("rep", None)),
        out_specs=P(("shuf", "rep"), None),
        check_vma=False,
    )
```

time: 161 us -> 61.4 us (0.38)
  Pallas kernels: 0 us -> 55.3 us
  blocking collectives: 52 us -> 0 us
  waiting for transfers between devices: 41.4 us -> 0 us
  starting transfers between devices: 30.1 us -> 0 us
  other arithmetic: 14 us -> 0 us
  matrix products: 10.2 us -> 0 us
  local copies, waits for them, and re-layouts: 11.8 us -> 5.89 us
    pallas_call x0 -> x2, Pallas kernels: none -> 55.3 us  [the longest x1 53.3 us: on_device(): pl.pallas_call(exchange, out_shape=pltpu.VMEM((OROWS, OUT), BF16), in_spe...]
    all_to_all x1 -> x0, blocking collectives: 52 us -> none  [on_device(): lax.all_to_all(standard, 'rep', split_axis=0, concat_axis=1, tiled=True)]
    all_to_all x4 -> x0, waiting for transfers between devices: 41.4 us -> none  [the longest x2 20.6 us: from_everyone(): lax.all_to_all(jnp.broadcast_to(value[None], (peers, *value.shape)), axis...]
    all_to_all x4 -> x0, starting transfers between devices: 30.1 us -> none  [the longest x2 16.9 us: from_everyone(): lax.all_to_all(jnp.broadcast_to(value[None], (peers, *value.shape)), axis...]
    dot_general x7 -> x0, matrix products: 10.2 us -> none  [the longest x4 9.55 us: on_device(): jnp.dot(full_rows[:, block * local_cols:(block + 1) * local_cols], full_w...]
    reduce_sum x5 -> x0, other arithmetic: 8.39 us -> none  [the longest x1 4.64 us: on_device(): tile_sum = jnp.sum(widened, axis=1)]
    all_to_all x4 -> x0, local copies, waits for them, and re-layouts: 7.1 us -> none  [the longest x1 6.2 us: on_device(): lax.all_to_all(standard, 'rep', split_axis=0, concat_axis=1, tiled=True)]
    unnamed x12, local copies, waits for them, and re-layouts: 0.03 us -> 5.89 us
  transfers between devices with their start and end apart: 4 -> 0, of which waited for: 4 -> 0; matrix products, arithmetic and copies ran while one was open for 9% -> 0% of each run, Pallas kernels for 0% -> 0%
where the time goes in v1:
time: 61.4 us; the launch traced here: 61.2 us
  Pallas kernels  55.3 us (90%)
  local copies, waits for them, and re-layouts  5.89 us (10%)
    pallas_call x1, Pallas kernels, on_device(): pl.pallas_call(exchange, out_shape=pltpu.VMEM((OROWS, OUT), BF16), in_spe...  53.3 us
    unnamed x12, local copies, waits for them, and re-layouts  5.89 us
    pallas_call x1, Pallas kernels, on_device(): pl.pallas_call(write_out, out_shape=jax.ShapeDtypeStruct((OROWS, OUT), BF...  2.04 us

profile of v1, /device:TPU:1, one launch (start us, length us, event | category | flops | bytes accessed | tf_op | source)
XLA Modules:
  0.0 61.2 jit_solution(5762910324632061400)
XLA Ops:
  0.0 0.0 copy-start
  0.0 2.2 %copy-done = bf16[8192,256]{1,0:T(8,128)(2,1)S(1)} copy-done((bf16[8192,256]{1,0:T(8,128)(2,1)S(1)}, bf16[8192,256]{1,0:T(8,128)(2,1)}, u32[]{:S(2)}) %copy-start) | copy-done | bytes 4194328
  2.2 0.0 copy-start.1
  2.2 1.0 %copy-done.1 = bf16[256,1024]{1,0:T(8,128)(2,1)S(1)} copy-done((bf16[256,1024]{1,0:T(8,128)(2,1)S(1)}, bf16[256,1024]{1,0:T(8,128)(2,1)}, u32[]{:S(2)}) %copy-start.1) | copy-done | bytes 524312
  3.2 0.0 copy-start.2
  3.2 0.7 %copy-done.2 = f32[256]{0:T(256)S(1)} copy-done((f32[256]{0:T(256)S(1)}, f32[256]{0:T(256)}, u32[]{:S(2)}) %copy-start.2) | copy-done | bytes 1048
  3.9 0.0 copy-start.3
  3.9 0.7 %copy-done.3 = f32[256]{0:T(256)S(1)} copy-done((f32[256]{0:T(256)S(1)}, f32[256]{0:T(256)}, u32[]{:S(2)}) %copy-start.3) | copy-done | bytes 1048
  4.6 0.0 copy-start.4
  4.6 0.7 %copy-done.4 = s32[64]{0:T(128)S(1)} copy-done((s32[64]{0:T(128)S(1)}, s32[64]{0:T(128)}, u32[]{:S(2)}) %copy-start.4) | copy-done | bytes 280
  5.2 0.0 copy-start.5
  5.2 0.7 %copy-done.5 = s32[64,1]{0,1:T(1,128)S(1)} copy-done((s32[64,1]{0,1:T(1,128)S(1)}, s32[64,1]{0,1:T(1,128)}, u32[]{:S(2)}) %copy-start.5) | copy-done | bytes 280
  5.9 53.3 %shard_map.64.src = bf16[2048,1024]{1,0:T(8,128)(2,1)S(1)} custom-call(bf16[8192,256]{1,0:T(8,128)(2,1)S(1)} %copy-done, s32[64]{0:T(128)S(1)} %copy-done.4, s32[64]{0:T(128)S(1)} %bitcast.1, f32[256]{0:T(256)S(1)} %copy-done.2, f32[256]{0:T(256)S(1)} %copy-done.3, bf16[256,1024]{1,0:T(8,128)(2,1)S(1)} %copy-done.1), custom_call_target="tpu_custom_call" | custom-call | tf_op jit(solution)/shard_map/pallas_call | solution.py:327
  59.2 2.0 %shard_map.65 = bf16[2048,1024]{1,0:T(8,128)(2,1)} custom-call(bf16[2048,1024]{1,0:T(8,128)(2,1)S(1)} %shard_map.64.src), custom_call_target="tpu_custom_call" | custom-call | tf_op jit(solution)/shard_map/pallas_call | solution.py:364
Async XLA Ops:
  0.0 2.2 %copy-start = (bf16[8192,256]{1,0:T(8,128)(2,1)S(1)}, bf16[8192,256]{1,0:T(8,128)(2,1)}, u32[]{:S(2)}) copy-start(bf16[8192,256]{1,0:T(8,128)(2,1)} %values.1) | copy-start | bytes 12582916
  2.2 1.0 %copy-start.1 = (bf16[256,1024]{1,0:T(8,128)(2,1)S(1)}, bf16[256,1024]{1,0:T(8,128)(2,1)}, u32[]{:S(2)}) copy-start(bf16[256,1024]{1,0:T(8,128)(2,1)} %weight.1) | copy-start | bytes 1572868
  3.2 0.7 %copy-start.2 = (f32[256]{0:T(256)S(1)}, f32[256]{0:T(256)}, u32[]{:S(2)}) copy-start(f32[256]{0:T(256)} %gain.1) | copy-start | bytes 3076
  3.9 0.7 %copy-start.3 = (f32[256]{0:T(256)S(1)}, f32[256]{0:T(256)}, u32[]{:S(2)}) copy-start(f32[256]{0:T(256)} %bias.1) | copy-start | bytes 3076
  4.6 0.7 %copy-start.4 = (s32[64]{0:T(128)S(1)}, s32[64]{0:T(128)}, u32[]{:S(2)}) copy-start(s32[64]{0:T(128)} %subgroup.1) | copy-start | bytes 772
  5.2 0.7 %copy-start.5 = (s32[64,1]{0,1:T(1,128)S(1)}, s32[64,1]{0,1:T(1,128)}, u32[]{:S(2)}) copy-start(s32[64,1]{0,1:T(1,128)} %param.8) | copy-start | bytes 772

commit v2 on v1

--- a/solution.py
+++ b/solution.py
@@ -360,7 +360,7 @@
         compiler_params=pltpu.CompilerParams(
             collective_id=0, has_side_effects=True, vmem_limit_bytes=32 * 1024 * 1024
         ),
-    )(values, subgroup, owners.reshape(TILES), col_gain, col_bias, out_weight)
+    )(*(pltpu.with_memory_space_constraint(a, pltpu.HBM) for a in (values, subgroup, owners.reshape(TILES), col_gain, col_bias, out_weight)))
     return pl.pallas_call(
         write_out,
         out_shape=jax.ShapeDtypeStruct((OROWS, OUT), BF16),

time: 61.4 us -> 55 us (0.90)
  local copies, waits for them, and re-layouts: 5.89 us -> 0 us
    unnamed x12 -> x0, local copies, waits for them, and re-layouts: 5.89 us -> none
where the time goes in v2:
time: 55 us
  Pallas kernels  55 us (100%)
    pallas_call x1, Pallas kernels, on_device(): pl.pallas_call(exchange, out_shape=pltpu.VMEM((OROWS, OUT), BF16), in_spe...  52.9 us
    pallas_call x1, Pallas kernels, on_device(): pl.pallas_call(write_out, out_shape=jax.ShapeDtypeStruct((OROWS, OUT), BF...  2.04 us

profile of v2, /device:TPU:1, one launch (start us, length us, event | category | flops | bytes accessed | tf_op | source)
XLA Modules:
  0.0 55.0 jit_solution(7334988048883638359)
XLA Ops:
  0.0 52.9 %shard_map.64.src = bf16[2048,1024]{1,0:T(8,128)(2,1)S(1)} custom-call(bf16[8192,256]{1,0:T(8,128)(2,1)} %values.1, s32[64]{0:T(128)} %subgroup.1, s32[64]{0:T(128)} %bitcast.1, f32[256]{0:T(256)} %gain.1, f32[256]{0:T(256)} %bias.1, bf16[256,1024]{1,0:T(8,128)(2,1)} %weight.1), custom_call_target="tpu_custom_call" | custom-call | tf_op jit(solution)/shard_map/pallas_call | solution.py:327
  52.9 2.0 %shard_map.65 = bf16[2048,1024]{1,0:T(8,128)(2,1)} custom-call(bf16[2048,1024]{1,0:T(8,128)(2,1)S(1)} %shard_map.64.src), custom_call_target="tpu_custom_call" | custom-call | tf_op jit(solution)/shard_map/pallas_call | solution.py:364

commit v3 on v2

v3 whole, which is shorter than its diff:
```python
import jax
import jax.numpy as jnp
from jax import lax
from jax.experimental import pallas as pl
from jax.experimental.pallas import tpu as pltpu
from jax.sharding import PartitionSpec as P

TILE = 128
TILES = 64
GRP_DEV = 32
PRIOR = 256.0
COLS = 256
OUT = 1024
ROWS = 8192
OROWS = 2048
NX, NY, NZ, NC = 4, 4, 8, 2
NQ = NY * NC
SLOTS = 2 * NQ * NZ
GROWS = 256
PIECES = (512, 512, 512, 256, 128, 128)
STARTS = tuple(sum(PIECES[:k]) for k in range(len(PIECES)))
LAST = PIECES[-1]
KEPT = OROWS - LAST
EARLY = 3
HEAD = 1
ORDER = ((2, 2), (1, 1), (3, 3))
MSG = 2 * COLS + 128
MESH = pl.DeviceIdType.MESH
F32, BF16 = jnp.float32, jnp.bfloat16


def shuf_index(y, z, c):
    return (y * NZ + z) * NC + c


def iota(shape, dim):
    return lax.broadcasted_iota(jnp.int32, shape, dim)


def pick(matrix, rows):
    return jnp.dot(matrix, rows, preferred_element_type=F32)


def standardized(v, par, gb, t, d):
    cols = slice(d * COLS, (d + 1) * COLS)
    scored = (v.astype(F32) - par[0, pl.ds(t, 1), cols]) * par[1, pl.ds(t, 1), cols]
    return (scored + gb[d, 1:2, :]).astype(BF16)


def exchange(
    values, subgroup, owners, gain, bias, weight,
    out, last, own_last, wall, par, gb,
    vals, raw, subs, owns, tstat, totals, tot_y, tot_z,
    send_y, buf_y, send_z, buf_z, back_z, got_z, back_y, got_y, tile_stat, peer_stat, lhs,
    load_sem, aux_sem, x_send, x_recv, wx_send, wx_recv, wz_send, wz_recv, wy_send, wy_recv,
    wc_send, wc_recv, gb_send, gb_recv, st_send, st_recv, line_send, line_recv, near, lines, far,
):
    shuf, x = lax.axis_index("shuf"), lax.axis_index("rep")
    y, z, c = shuf // (NZ * NC), lax.rem(shuf // NC, NZ), lax.rem(shuf, NC)
    q = y * NC + c
    barrier = pltpu.get_barrier_semaphore()

    def x_peer(d):
        return (shuf, lax.rem(x + d, NX))

    def z_peer(d):
        return (shuf_index(y, lax.rem(z + d, NZ), c), x)

    def q_peer(d):
        p = lax.rem(q + d, NQ)
        return (shuf_index(p // NC, z, lax.rem(p, NC)), x)

    def signal(sem, to):
        pl.semaphore_signal(sem, inc=1, device_id=to, device_id_type=MESH)

    def send(src, dst, s, r, to):
        pltpu.make_async_remote_copy(src, dst, s, r, device_id=to, device_id_type=MESH).start()

    def wait_for(ref, sem):
        pltpu.make_async_copy(ref, ref, sem).wait()

    loads = []
    for i in range(8):
        part = pl.ds(i * 1024, 1024)
        loads.append(pltpu.make_async_copy(values.at[part], vals.at[part], load_sem.at[i]))
        loads[-1].start()
    aux = [
        pltpu.make_async_copy(subgroup, subs, aux_sem.at[0]),
        pltpu.make_async_copy(owners, owns, aux_sem.at[1]),
        pltpu.make_async_copy(weight, wall.at[pl.ds(0, COLS)], aux_sem.at[2]),
        pltpu.make_async_copy(gain, gb.at[0, 0], aux_sem.at[3]),
        pltpu.make_async_copy(bias, gb.at[0, 1], aux_sem.at[4]),
    ]
    for a in aux:
        a.start()

    is_head = x == HEAD

    @pl.when(is_head)
    def _():
        for d in range(1, NX):
            signal(barrier, x_peer(d))
        for d in range(1, NQ):
            signal(barrier, q_peer(d))
        for d in range(1, NZ):
            signal(barrier, z_peer(d))

    @pl.when(x != HEAD)
    def _():
        for d in range(1, NX):
            @pl.when(lax.rem(x + d, NX) != HEAD)
            def _():
                signal(barrier, x_peer(d))
        pl.semaphore_wait(barrier, NX - 1)
        signal(near, (shuf, HEAD))

    @pl.when(is_head)
    def _():
        pl.semaphore_wait(near, NX - 1)

    gathers = c == NC - 1
    w_cols = pl.ds(pl.multiple_of(y * 256, 256), 256)

    def w_rows(block):
        return pl.ds(pl.multiple_of(block * COLS + z * 32, 32), 32)

    for d in range(1, NX):
        at = NX - d
        send(gain, gb.at[at, 0], gb_send, gb_recv, x_peer(d))
        send(bias, gb.at[at, 1], gb_send, gb_recv, x_peer(d))

    @pl.when(gathers)
    def _():
        for d in range(1, NX):
            send(
                weight.at[w_rows(0), w_cols], wall.at[w_rows(NX - d), w_cols],
                wx_send, wx_recv, x_peer(d),
            )

    late_half = x // 2

    def send_piece(k):
        size = PIECES[k]
        for one, other in ORDER:
            d = one + (other - one) * late_half
            at = NX - 1 - d
            first = lax.rem(x + d, NX) * OROWS + STARTS[k]
            send(
                values.at[pl.ds(pl.multiple_of(first, LAST), size)],
                last.at[at] if k == len(PIECES) - 1 else raw.at[at, pl.ds(STARTS[k], size)],
                x_send.at[k // (len(PIECES) - 1)], x_recv.at[at, k], x_peer(d),
            )

    for k in range(EARLY):
        send_piece(k)

    @pl.when(is_head)
    def _():
        pl.semaphore_wait(barrier, NQ - 1 + NZ - 1)
        for d in range(1, NQ):
            signal(lines.at[0], q_peer(d))
        for d in range(1, NZ):
            signal(lines.at[1], z_peer(d))

    @pl.loop(0, 8)
    def _(i):
        wait_for(vals.at[pl.ds(0, 1024)], load_sem.at[i])

        @pl.loop(0, 8)
        def _(j):
            t = i * 8 + j
            a = jnp.zeros((8, COLS), F32)
            b = jnp.zeros((8, COLS), F32)
            for k in range(TILE // 16):
                v = vals[pl.ds(pl.multiple_of(t * TILE + k * 16, 16), 16), :].astype(F32)
                lo, hi = v[:8], v[8:]
                a = a + lo + hi
                b = b + lo * lo + hi * hi
            tstat[pl.ds(t, 1), :COLS] = jnp.sum(a, axis=0, keepdims=True)
            tstat[pl.ds(t, 1), COLS:] = jnp.sum(b, axis=0, keepdims=True)

    sums = tstat[...]
    own_total = jnp.sum(sums, axis=0, keepdims=True)
    totals[0] = own_total
    tot_y[q] = own_total

    for a in aux[:2]:
        a.wait()
    lane = iota((8, TILES), 1)
    own_row = jnp.zeros((8, TILES), jnp.int32)
    sub_row = jnp.zeros((8, TILES), jnp.int32)
    for t in range(TILES):
        own_row = jnp.where(lane == t, owns[t], own_row)
        sub_row = jnp.where(lane == t, subs[t], sub_row)
    i0, i1 = iota((TILES, TILES), 0), iota((TILES, TILES), 1)
    eye = i0 == i1

    def as_rows(row):
        return jnp.broadcast_to(row[:1], (TILES, TILES))

    def as_column(row):
        spread = jnp.where(eye, as_rows(row), 0).astype(F32)
        return jnp.sum(spread, axis=1, keepdims=True).astype(jnp.int32)

    same = (as_rows(own_row) == as_column(own_row)) & (i0 < i1)
    pos = jnp.sum(jnp.where(same, 1.0, 0.0), axis=0, keepdims=True).astype(jnp.int32)
    o = own_row[:1]
    slot = ((((o >> 4) * NC + (o & 1)) * NZ + ((o >> 1) & 7)) * 2) + pos
    slot_col = as_column(slot)
    to_slot = jnp.where(iota((SLOTS, TILES), 0) == slot, 1.0, 0.0).astype(BF16)
    from_slot = jnp.where(iota((TILES, SLOTS), 1) == slot_col, 1.0, 0.0).astype(BF16)
    label = jnp.where(iota((TILES, 128), 1) == as_column(sub_row), 1.0, 0.0).astype(BF16)
    packed = jnp.concatenate([sums.astype(BF16), label], axis=1)
    send_y[...] = pick(to_slot, packed).astype(BF16).reshape(NQ, 16, MSG)
    buf_y[q] = send_y[q]

    r0, r1 = iota((SLOTS, SLOTS), 0), iota((SLOTS, SLOTS), 1)
    swap = jnp.where(r1 == ((r0 >> 1) & 7) * 16 + (r0 >> 4) * 2 + (r0 & 1), 1.0, 0.0).astype(BF16)

    def line_known(i, peers):
        @pl.when(is_head)
        def _():
            pl.semaphore_wait(lines.at[i], peers)
            for d in range(1, NX):
                signal(far.at[i], x_peer(d))

        @pl.when(x != HEAD)
        def _():
            pl.semaphore_wait(far.at[i], 1)

    line_known(0, NQ - 1)
    for d in range(1, NQ):
        p = lax.rem(q + d, NQ)
        send(totals.at[0], tot_y.at[q], line_send.at[0], line_recv.at[0], q_peer(d))
        send(send_y.at[p], buf_y.at[q], line_send.at[1], line_recv.at[1], q_peer(d))

    line_known(1, NZ - 1)
    wx_all = wall.at[pl.ds(0, (NX - 1) * 32), pl.ds(0, 256)]
    wz_all = wall.at[pl.ds(0, (NX - 1) * (NZ - 1) * 32), pl.ds(0, 256)]
    wy_all = wall.at[pl.ds(0, (NX - 1) * COLS), pl.ds(0, 768)]
    foreign = wall.at[pl.ds(COLS, (NX - 1) * COLS)]

    @pl.when(gathers)
    def _():
        wait_for(wx_all, wx_recv)
        for d in range(1, NZ):
            for b in range(1, NX):
                piece = wall.at[w_rows(b), w_cols]
                send(piece, piece, wz_send, wz_recv, z_peer(d))

    wait_for(tot_y.at[pl.ds(0, NQ - 1)], line_recv.at[0])
    wait_for(buf_y.at[pl.ds(0, NQ - 1)], line_recv.at[1])
    line_total = jnp.sum(tot_y[...], axis=0)
    totals[1] = line_total
    tot_z[z] = line_total
    send_z[...] = pick(swap, buf_y[...].reshape(SLOTS, MSG)).astype(BF16).reshape(NZ, 16, MSG)
    buf_z[z] = send_z[z]
    for d in range(1, NZ):
        p = lax.rem(z + d, NZ)
        send(totals.at[1], tot_z.at[z], line_send.at[2], line_recv.at[2], z_peer(d))
        send(send_z.at[p], buf_z.at[z], line_send.at[3], line_recv.at[3], z_peer(d))

    @pl.when(gathers)
    def _():
        wait_for(wz_all, wz_recv)
        for d in range(1, NY):
            for b in range(1, NX):
                piece = wall.at[pl.ds(b * COLS, COLS), w_cols]
                send(piece, piece, wy_send, wy_recv, q_peer(NC * d))

    wait_for(tot_z.at[pl.ds(0, NZ - 1)], line_recv.at[2])
    wait_for(buf_z.at[pl.ds(0, NZ - 1)], line_recv.at[3])
    total = jnp.sum(tot_z[...], axis=0) / float(ROWS * NQ * NZ)
    arrived = buf_z[...].reshape(SLOTS, MSG)
    member = arrived[:, 2 * COLS:]
    member_t = jnp.transpose(member.astype(F32))[:GRP_DEV].astype(BF16)
    group = pick(member_t, arrived[:, : 2 * COLS])
    count = float(TILE) * jnp.sum(member_t.astype(F32), axis=1, keepdims=True)
    blended = (group + PRIOR * total) / (count + PRIOR)
    center, second = blended[:, :COLS], blended[:, COLS:]
    inverse = lax.rsqrt(second - center * center + 1e-05)
    both = jnp.concatenate([center, inverse], axis=1).astype(BF16)
    both = jnp.concatenate([both, jnp.zeros((128 - GRP_DEV, 2 * COLS), BF16)], axis=0)
    back_z[...] = pick(member, both).astype(BF16).reshape(NZ, 16, 2 * COLS)
    got_z[z] = back_z[z]
    for d in range(1, NZ):
        p = lax.rem(z + d, NZ)
        send(back_z.at[p], got_z.at[z], line_send.at[4], line_recv.at[4], z_peer(d))

    wait_for(got_z.at[pl.ds(0, NZ - 1)], line_recv.at[4])
    back_y[...] = pick(swap, got_z[...].reshape(SLOTS, 2 * COLS)).astype(BF16).reshape(NQ, 16, 2 * COLS)
    got_y[q] = back_y[q]
    for d in range(1, NQ):
        p = lax.rem(q + d, NQ)
        send(back_y.at[p], got_y.at[q], line_send.at[5], line_recv.at[5], q_peer(d))

    @pl.when(gathers)
    def _():
        wait_for(wy_all, wy_recv)
        send(foreign, foreign, wc_send, wc_recv, (shuf_index(y, z, 0), x))

    wait_for(got_y.at[pl.ds(0, NQ - 1)], line_recv.at[5])
    tile_stat[...] = pick(from_slot, got_y[...].reshape(SLOTS, 2 * COLS)).astype(BF16)
    for d in range(1, NX):
        rows = pl.ds(pl.multiple_of(lax.rem(x + d, NX) * 16, 16), 16)
        send(tile_stat.at[rows], peer_stat.at[NX - d - 1], st_send, st_recv, x_peer(d))
    for k in range(EARLY, len(PIECES)):
        send_piece(k)

    for a in aux[2:]:
        a.wait()
    wait_for(gb.at[pl.ds(0, NX - 1)], gb_recv)

    @pl.when(c == 0)
    def _():
        wait_for(foreign, wc_recv)

    own_rows = pl.ds(pl.multiple_of(x * 16, 16), 16)
    stats = [tile_stat[own_rows, :]]
    wait_for(peer_stat, st_recv)
    stats += [peer_stat[d] for d in range(NX - 1)]
    for d in range(NX):
        s = stats[d].astype(F32)
        par[0, :, d * COLS:(d + 1) * COLS] = s[:, :COLS]
        par[1, :, d * COLS:(d + 1) * COLS] = s[:, COLS:] * gb[d, 0:1, :]

    def own_scored(t):
        first = x * OROWS + t * TILE
        v = vals[pl.ds(pl.multiple_of(first, TILE), TILE), :]
        return standardized(v, par, gb, t, 0)

    def arrived_piece(k):
        for d in range(NX - 1):
            wait_for(last.at[d] if k == len(PIECES) - 1 else raw.at[d, pl.ds(0, PIECES[k])], x_recv.at[d, k])

    def project(first, count):
        for j in range(count // TILE):
            t = first // TILE + j
            at = slice(j * TILE, (j + 1) * TILE)
            lhs[at, :COLS] = own_scored(t)
            for d in range(1, NX):
                v = raw[d - 1, pl.ds(pl.multiple_of(t * TILE, TILE), TILE), :]
                lhs[at, d * COLS:(d + 1) * COLS] = standardized(v, par, gb, t, d)
        rows = pl.ds(pl.multiple_of(first, count), count)
        out[rows, :] = jnp.dot(lhs[:count, :], wall[...], preferred_element_type=F32).astype(BF16)

    for k in range(EARLY):
        arrived_piece(k)

    @pl.loop(0, STARTS[EARLY + 1] // GROWS)
    def _(g):
        @pl.when(g == STARTS[EARLY] // GROWS)
        def _():
            arrived_piece(EARLY)

        project(g * GROWS, GROWS)

    own_last[...] = own_scored(KEPT // TILE)
    arrived_piece(EARLY + 1)
    project(STARTS[EARLY + 1], PIECES[EARLY + 1])
    arrived_piece(EARLY + 2)

    wait_for(raw, x_send.at[0])
    wait_for(last, x_send.at[1])

    @pl.when(gathers)
    def _():
        wait_for(wx_all, wx_send)
        wait_for(wz_all, wz_send)
        wait_for(wy_all, wy_send)
        wait_for(foreign, wc_send)

    wait_for(gb.at[pl.ds(0, NX - 1)], gb_send)
    wait_for(peer_stat, st_send)
    wait_for(tot_y.at[pl.ds(0, NQ - 1)], line_send.at[0])
    wait_for(buf_y.at[pl.ds(0, NQ - 1)], line_send.at[1])
    wait_for(tot_z.at[pl.ds(0, NZ - 1)], line_send.at[2])
    wait_for(buf_z.at[pl.ds(0, NZ - 1)], line_send.at[3])
    wait_for(got_z.at[pl.ds(0, NZ - 1)], line_send.at[4])
    wait_for(got_y.at[pl.ds(0, NQ - 1)], line_send.at[5])


def finish(done, last, own_last, wall, par, gb, dst, lhs, rows, sem):
    early = pltpu.make_async_copy(done, dst.at[pl.ds(0, KEPT)], sem.at[0])
    early.start()
    lhs[:, :COLS] = own_last[...]
    for d in range(1, NX):
        lhs[:, d * COLS:(d + 1) * COLS] = standardized(last[d - 1], par, gb, KEPT // TILE, d)
    rows[...] = jnp.dot(lhs[...], wall[...], preferred_element_type=F32).astype(BF16)
    late = pltpu.make_async_copy(rows, dst.at[pl.ds(KEPT, LAST)], sem.at[1])
    late.start()
    early.wait()
    late.wait()


def on_device(values, subgroup, owners, col_gain, col_bias, out_weight):
    dma, vmem = pltpu.SemaphoreType.DMA, pltpu.VMEM
    hbm = pl.BlockSpec(memory_space=pltpu.HBM)
    results = [
        vmem((KEPT, OUT), BF16),
        vmem((NX - 1, LAST, COLS), BF16),
        vmem((LAST, COLS), BF16),
        vmem((NX * COLS, OUT), BF16),
        vmem((2, 16, NX * COLS), F32),
        vmem((NX, 2, COLS), F32),
    ]
    in_vmem = [pl.BlockSpec(memory_space=vmem)] * len(results)
    held = pl.pallas_call(
        exchange,
        out_shape=results,
        in_specs=[hbm] * 6,
        out_specs=in_vmem,
        scratch_shapes=[
            vmem((ROWS, COLS), BF16),
            vmem((NX - 1, KEPT, COLS), BF16),
            pltpu.SMEM((TILES,), jnp.int32),
            pltpu.SMEM((TILES,), jnp.int32),
            vmem((TILES, 2 * COLS), F32),
            vmem((2, 1, 2 * COLS), F32),
            vmem((NQ, 1, 2 * COLS), F32),
            vmem((NZ, 1, 2 * COLS), F32),
            vmem((NQ, 16, MSG), BF16),
            vmem((NQ, 16, MSG), BF16),
            vmem((NZ, 16, MSG), BF16),
            vmem((NZ, 16, MSG), BF16),
            vmem((NZ, 16, 2 * COLS), BF16),
            vmem((NZ, 16, 2 * COLS), BF16),
            vmem((NQ, 16, 2 * COLS), BF16),
            vmem((NQ, 16, 2 * COLS), BF16),
            vmem((TILES, 2 * COLS), BF16),
            vmem((NX - 1, 16, 2 * COLS), BF16),
            vmem((GROWS, NX * COLS), BF16),
            dma((8,)), dma((5,)), dma((2,)), dma((NX - 1, len(PIECES))),
            dma, dma, dma, dma, dma, dma, dma, dma, dma, dma, dma, dma,
            dma((6,)), dma((6,)),
            pltpu.SemaphoreType.REGULAR,
            pltpu.SemaphoreType.REGULAR((2,)), pltpu.SemaphoreType.REGULAR((2,)),
        ],
        compiler_params=pltpu.CompilerParams(
            collective_id=0, has_side_effects=True, vmem_limit_bytes=32 * 1024 * 1024
        ),
    )(*(
        pltpu.with_memory_space_constraint(a, pltpu.HBM)
        for a in (values, subgroup, owners.reshape(TILES), col_gain, col_bias, out_weight)
    ))
    return pl.pallas_call(
        finish,
        out_shape=jax.ShapeDtypeStruct((OROWS, OUT), BF16),
        in_specs=in_vmem,
        out_specs=hbm,
        scratch_shapes=[vmem((LAST, NX * COLS), BF16), vmem((LAST, OUT), BF16), dma((2,))],
        compiler_params=pltpu.CompilerParams(vmem_limit_bytes=8 * 1024 * 1024),
    )(*held)


def solution(mesh):
    return jax.shard_map(
        on_device,
        mesh=mesh,
        in_specs=(P("shuf", "rep"), P("shuf"), P("shuf", None), P("rep"), P("rep"), P("rep", None)),
        out_specs=P(("shuf", "rep"), None),
        check_vma=False,
    )
```

time: 55 us -> 54.4 us (0.989)
  Pallas kernels: 55 us -> 54.2 us
    pallas_call x2, Pallas kernels: 55 us -> 54.2 us  [the longest x1 52.2 us: on_device(): pl.pallas_call(exchange, out_shape=results, in_specs=[hbm] * 6, out_specs...]
where the time goes in v3:
time: 54.4 us; the launch traced here: 54.2 us
  Pallas kernels  54.2 us (100%)
    pallas_call x1, Pallas kernels, on_device(): pl.pallas_call(exchange, out_shape=results, in_specs=[hbm] * 6, out_specs...  52.2 us
    pallas_call x1, Pallas kernels, on_device(): pl.pallas_call(finish, out_shape=jax.ShapeDtypeStruct((OROWS, OUT), BF16)...  2.02 us

profile of v3, /device:TPU:1, one launch (start us, length us, event | category | flops | bytes accessed | tf_op | source)
XLA Modules:
  0.0 54.2 jit_solution(2282459579000381820)
XLA Ops:
  0.0 52.2 %shard_map.64 = (bf16[1920,1024]{1,0:T(8,128)(2,1)S(1)}, bf16[3,128,256]{2,1,0:T(8,128)(2,1)S(1)}, bf16[128,256]{1,0:T(8,128)(2,1)S(1)}, bf16[1024,1024]{1,0:T(8...) custom-call(bf16[8192,256]{1,0:T(8,128)(2,1)} %values.1, s32[64]{0:T(128)} %subgroup.1, s32[64]{0:T(128)} %bitcast.1, ...), custom_call_target="tpu_custom_call" | custom-call | tf_op jit(solution)/shard_map/pallas_call | solution.py:408
  52.2 2.0 %shard_map.65 = bf16[2048,1024]{1,0:T(8,128)(2,1)} custom-call(bf16[1920,1024]{1,0:T(8,128)(2,1)S(1)} %get-tuple-element.11.done, bf16[3,128,256]{2,1,0:T(8,128)(2,1)S(1)} %get-tuple-element.12.last, bf16[128,256]{1,0:T(8,128)(2,1)S(1)} %get-tuple-element.13.own_last, bf16[1024,1024]{1,0:T(8,128)(2,1)S(1)} %get-tuple-element.14.wall, ...), custom_call_target="tpu_custom_call" | custom-call | tf_op jit(solution)/shard_map/pallas_call | solution.py:446

commit v4 on v3

--- a/solution.py
+++ b/solution.py
@@ -16,15 +16,20 @@
 NX, NY, NZ, NC = 4, 4, 8, 2
 NQ = NY * NC
 SLOTS = 2 * NQ * NZ
+MSG = 2 * COLS + 128
 GROWS = 256
 PIECES = (512, 512, 512, 256, 128, 128)
 STARTS = tuple(sum(PIECES[:k]) for k in range(len(PIECES)))
 LAST = PIECES[-1]
 KEPT = OROWS - LAST
+SENT_BYTES = 2 * (
+    (NX - 1) * (OROWS * COLS + 16 * 2 * COLS)
+    + (NQ - 1 + NZ - 1) * 16 * (MSG + 2 * COLS)
+)
+W_BYTES = 2 * 256 * (NX - 1) * (32 + (NZ - 1) * 32 + (NY - 1) * COLS + 4 * COLS)
 EARLY = 3
 HEAD = 1
 ORDER = ((2, 2), (1, 1), (3, 3))
-MSG = 2 * COLS + 128
 MESH = pl.DeviceIdType.MESH
 F32, BF16 = jnp.float32, jnp.bfloat16
 
@@ -50,15 +55,16 @@
 def exchange(
     values, subgroup, owners, gain, bias, weight,
     out, last, own_last, wall, par, gb,
-    vals, raw, subs, owns, tstat, totals, tot_y, tot_z,
+    vals, raw, subs, owns, tstat, totals, tots,
     send_y, buf_y, send_z, buf_z, back_z, got_z, back_y, got_y, tile_stat, peer_stat, lhs,
-    load_sem, aux_sem, x_send, x_recv, wx_send, wx_recv, wz_send, wz_recv, wy_send, wy_recv,
-    wc_send, wc_recv, gb_send, gb_recv, st_send, st_recv, line_send, line_recv, near, lines, far,
+    load_sem, slot_sem, own_sem, sent, tot_sent, gb_sent, w_sent,
+    x_recv, wx_recv, wz_recv, wy_recv, wc_recv, gb_recv, st_recv, line_recv, near, lines, far,
 ):
     shuf, x = lax.axis_index("shuf"), lax.axis_index("rep")
     y, z, c = shuf // (NZ * NC), lax.rem(shuf // NC, NZ), lax.rem(shuf, NC)
     q = y * NC + c
     barrier = pltpu.get_barrier_semaphore()
+    tot_y, tot_z = tots.at[pl.ds(0, NQ)], tots.at[pl.ds(NQ, NZ)]
 
     def x_peer(d):
         return (shuf, lax.rem(x + d, NX))
@@ -79,17 +85,13 @@
     def wait_for(ref, sem):
         pltpu.make_async_copy(ref, ref, sem).wait()
 
-    loads = []
-    for i in range(8):
-        part = pl.ds(i * 1024, 1024)
-        loads.append(pltpu.make_async_copy(values.at[part], vals.at[part], load_sem.at[i]))
-        loads[-1].start()
+    pltpu.make_async_copy(values, vals, load_sem).start()
     aux = [
-        pltpu.make_async_copy(subgroup, subs, aux_sem.at[0]),
-        pltpu.make_async_copy(owners, owns, aux_sem.at[1]),
-        pltpu.make_async_copy(weight, wall.at[pl.ds(0, COLS)], aux_sem.at[2]),
-        pltpu.make_async_copy(gain, gb.at[0, 0], aux_sem.at[3]),
-        pltpu.make_async_copy(bias, gb.at[0, 1], aux_sem.at[4]),
+        pltpu.make_async_copy(subgroup, subs, slot_sem.at[0]),
+        pltpu.make_async_copy(owners, owns, slot_sem.at[1]),
+        pltpu.make_async_copy(weight, wall.at[pl.ds(0, COLS)], own_sem),
+        pltpu.make_async_copy(gain, gb.at[0, 0], gb_recv),
+        pltpu.make_async_copy(bias, gb.at[0, 1], gb_recv),
     ]
     for a in aux:
         a.start()
@@ -126,15 +128,15 @@
 
     for d in range(1, NX):
         at = NX - d
-        send(gain, gb.at[at, 0], gb_send, gb_recv, x_peer(d))
-        send(bias, gb.at[at, 1], gb_send, gb_recv, x_peer(d))
+        send(gain, gb.at[at, 0], gb_sent, gb_recv, x_peer(d))
+        send(bias, gb.at[at, 1], gb_sent, gb_recv, x_peer(d))
 
     @pl.when(gathers)
     def _():
         for d in range(1, NX):
             send(
                 weight.at[w_rows(0), w_cols], wall.at[w_rows(NX - d), w_cols],
-                wx_send, wx_recv, x_peer(d),
+                w_sent, wx_recv, x_peer(d),
             )
 
     late_half = x // 2
@@ -148,7 +150,7 @@
             send(
                 values.at[pl.ds(pl.multiple_of(first, LAST), size)],
                 last.at[at] if k == len(PIECES) - 1 else raw.at[at, pl.ds(STARTS[k], size)],
-                x_send.at[k // (len(PIECES) - 1)], x_recv.at[at, k], x_peer(d),
+                sent, x_recv.at[max(k - EARLY + 1, 0)], x_peer(d),
             )
 
     for k in range(EARLY):
@@ -162,10 +164,10 @@
         for d in range(1, NZ):
             signal(lines.at[1], z_peer(d))
 
+    wait_for(vals, load_sem)
+
     @pl.loop(0, 8)
     def _(i):
-        wait_for(vals.at[pl.ds(0, 1024)], load_sem.at[i])
-
         @pl.loop(0, 8)
         def _(j):
             t = i * 8 + j
@@ -231,8 +233,8 @@
     line_known(0, NQ - 1)
     for d in range(1, NQ):
         p = lax.rem(q + d, NQ)
-        send(totals.at[0], tot_y.at[q], line_send.at[0], line_recv.at[0], q_peer(d))
-        send(send_y.at[p], buf_y.at[q], line_send.at[1], line_recv.at[1], q_peer(d))
+        send(totals.at[0], tot_y.at[q], tot_sent, line_recv.at[0], q_peer(d))
+        send(send_y.at[p], buf_y.at[q], sent, line_recv.at[1], q_peer(d))
 
     line_known(1, NZ - 1)
     wx_all = wall.at[pl.ds(0, (NX - 1) * 32), pl.ds(0, 256)]
@@ -246,7 +248,7 @@
         for d in range(1, NZ):
             for b in range(1, NX):
                 piece = wall.at[w_rows(b), w_cols]
-                send(piece, piece, wz_send, wz_recv, z_peer(d))
+                send(piece, piece, w_sent, wz_recv, z_peer(d))
 
     wait_for(tot_y.at[pl.ds(0, NQ - 1)], line_recv.at[0])
     wait_for(buf_y.at[pl.ds(0, NQ - 1)], line_recv.at[1])
@@ -257,8 +259,8 @@
     buf_z[z] = send_z[z]
     for d in range(1, NZ):
         p = lax.rem(z + d, NZ)
-        send(totals.at[1], tot_z.at[z], line_send.at[2], line_recv.at[2], z_peer(d))
-        send(send_z.at[p], buf_z.at[z], line_send.at[3], line_recv.at[3], z_peer(d))
+        send(totals.at[1], tot_z.at[z], tot_sent, line_recv.at[2], z_peer(d))
+        send(send_z.at[p], buf_z.at[z], sent, line_recv.at[3], z_peer(d))
 
     @pl.when(gathers)
     def _():
@@ -266,7 +268,7 @@
         for d in range(1, NY):
             for b in range(1, NX):
                 piece = wall.at[pl.ds(b * COLS, COLS), w_cols]
-                send(piece, piece, wy_send, wy_recv, q_peer(NC * d))
+                send(piece, piece, w_sent, wy_recv, q_peer(NC * d))
 
     wait_for(tot_z.at[pl.ds(0, NZ - 1)], line_recv.at[2])
     wait_for(buf_z.at[pl.ds(0, NZ - 1)], line_recv.at[3])
@@ -285,31 +287,30 @@
     got_z[z] = back_z[z]
     for d in range(1, NZ):
         p = lax.rem(z + d, NZ)
-        send(back_z.at[p], got_z.at[z], line_send.at[4], line_recv.at[4], z_peer(d))
+        send(back_z.at[p], got_z.at[z], sent, line_recv.at[4], z_peer(d))
 
     wait_for(got_z.at[pl.ds(0, NZ - 1)], line_recv.at[4])
     back_y[...] = pick(swap, got_z[...].reshape(SLOTS, 2 * COLS)).astype(BF16).reshape(NQ, 16, 2 * COLS)
     got_y[q] = back_y[q]
     for d in range(1, NQ):
         p = lax.rem(q + d, NQ)
-        send(back_y.at[p], got_y.at[q], line_send.at[5], line_recv.at[5], q_peer(d))
+        send(back_y.at[p], got_y.at[q], sent, line_recv.at[5], q_peer(d))
 
     @pl.when(gathers)
     def _():
         wait_for(wy_all, wy_recv)
-        send(foreign, foreign, wc_send, wc_recv, (shuf_index(y, z, 0), x))
+        send(foreign, foreign, w_sent, wc_recv, (shuf_index(y, z, 0), x))
 
     wait_for(got_y.at[pl.ds(0, NQ - 1)], line_recv.at[5])
     tile_stat[...] = pick(from_slot, got_y[...].reshape(SLOTS, 2 * COLS)).astype(BF16)
     for d in range(1, NX):
         rows = pl.ds(pl.multiple_of(lax.rem(x + d, NX) * 16, 16), 16)
-        send(tile_stat.at[rows], peer_stat.at[NX - d - 1], st_send, st_recv, x_peer(d))
+        send(tile_stat.at[rows], peer_stat.at[NX - d - 1], sent, st_recv, x_peer(d))
     for k in range(EARLY, len(PIECES)):
         send_piece(k)
 
-    for a in aux[2:]:
-        a.wait()
-    wait_for(gb.at[pl.ds(0, NX - 1)], gb_recv)
+    aux[2].wait()
+    wait_for(gb, gb_recv)
 
     @pl.when(c == 0)
     def _():
@@ -330,8 +331,9 @@
         return standardized(v, par, gb, t, 0)
 
     def arrived_piece(k):
-        for d in range(NX - 1):
-            wait_for(last.at[d] if k == len(PIECES) - 1 else raw.at[d, pl.ds(0, PIECES[k])], x_recv.at[d, k])
+        rows = STARTS[EARLY] if k < EARLY else PIECES[k]
+        whole = last if k == len(PIECES) - 1 else raw.at[:, pl.ds(0, rows)]
+        wait_for(whole, x_recv.at[max(k - EARLY + 1, 0)])
 
     def project(first, count):
         for j in range(count // TILE):
@@ -344,8 +346,7 @@
         rows = pl.ds(pl.multiple_of(first, count), count)
         out[rows, :] = jnp.dot(lhs[:count, :], wall[...], preferred_element_type=F32).astype(BF16)
 
-    for k in range(EARLY):
-        arrived_piece(k)
+    arrived_piece(0)
 
     @pl.loop(0, STARTS[EARLY + 1] // GROWS)
     def _(g):
@@ -360,24 +361,13 @@
     project(STARTS[EARLY + 1], PIECES[EARLY + 1])
     arrived_piece(EARLY + 2)
 
-    wait_for(raw, x_send.at[0])
-    wait_for(last, x_send.at[1])
+    wait_for(vals.at[pl.ds(0, SENT_BYTES // (2 * COLS))], sent)
+    wait_for(tots.at[pl.ds(0, NQ + NZ - 2)], tot_sent)
+    wait_for(gb.at[pl.ds(0, NX - 1)], gb_sent)
 
     @pl.when(gathers)
     def _():
-        wait_for(wx_all, wx_send)
-        wait_for(wz_all, wz_send)
-        wait_for(wy_all, wy_send)
-        wait_for(foreign, wc_send)
-
-    wait_for(gb.at[pl.ds(0, NX - 1)], gb_send)
-    wait_for(peer_stat, st_send)
-    wait_for(tot_y.at[pl.ds(0, NQ - 1)], line_send.at[0])
-    wait_for(buf_y.at[pl.ds(0, NQ - 1)], line_send.at[1])
-    wait_for(tot_z.at[pl.ds(0, NZ - 1)], line_send.at[2])
-    wait_for(buf_z.at[pl.ds(0, NZ - 1)], line_send.at[3])
-    wait_for(got_z.at[pl.ds(0, NZ - 1)], line_send.at[4])
-    wait_for(got_y.at[pl.ds(0, NQ - 1)], line_send.at[5])
+        wait_for(vals.at[pl.ds(0, W_BYTES // (2 * COLS))], w_sent)
 
 
 def finish(done, last, own_last, wall, par, gb, dst, lhs, rows, sem):
@@ -417,8 +407,7 @@
             pltpu.SMEM((TILES,), jnp.int32),
             vmem((TILES, 2 * COLS), F32),
             vmem((2, 1, 2 * COLS), F32),
-            vmem((NQ, 1, 2 * COLS), F32),
-            vmem((NZ, 1, 2 * COLS), F32),
+            vmem((NQ + NZ, 1, 2 * COLS), F32),
             vmem((NQ, 16, MSG), BF16),
             vmem((NQ, 16, MSG), BF16),
             vmem((NZ, 16, MSG), BF16),
@@ -430,9 +419,8 @@
             vmem((TILES, 2 * COLS), BF16),
             vmem((NX - 1, 16, 2 * COLS), BF16),
             vmem((GROWS, NX * COLS), BF16),
-            dma((8,)), dma((5,)), dma((2,)), dma((NX - 1, len(PIECES))),
-            dma, dma, dma, dma, dma, dma, dma, dma, dma, dma, dma, dma,
-            dma((6,)), dma((6,)),
+            dma, dma((2,)), dma, dma, dma, dma, dma,
+            dma((len(PIECES) - EARLY + 1,)), dma, dma, dma, dma, dma, dma, dma((6,)),
             pltpu.SemaphoreType.REGULAR,
             pltpu.SemaphoreType.REGULAR((2,)), pltpu.SemaphoreType.REGULAR((2,)),
         ],

time: 54.4 us -> 54.2 us (level)
  no operation moved by 1% of the time
where the time goes in v4:
time: 54.2 us; the launch traced here: 54.1 us
  Pallas kernels  54.1 us (100%)
    pallas_call x1, Pallas kernels, on_device(): pl.pallas_call(exchange, out_shape=results, in_specs=[hbm] * 6, out_specs...  52.1 us
    pallas_call x1, Pallas kernels, on_device(): pl.pallas_call(finish, out_shape=jax.ShapeDtypeStruct((OROWS, OUT), BF16)...  2.02 us

profile of v4, /device:TPU:1, one launch (start us, length us, event | category | flops | bytes accessed | tf_op | source)
XLA Modules:
  0.0 54.1 jit_solution(9646172139276166136)
XLA Ops:
  0.0 52.1 %shard_map.64 = (bf16[1920,1024]{1,0:T(8,128)(2,1)S(1)}, bf16[3,128,256]{2,1,0:T(8,128)(2,1)S(1)}, bf16[128,256]{1,0:T(8,128)(2,1)S(1)}, bf16[1024,1024]{1,0:T(8...) custom-call(bf16[8192,256]{1,0:T(8,128)(2,1)} %values.1, s32[64]{0:T(128)} %subgroup.1, s32[64]{0:T(128)} %bitcast.1, ...), custom_call_target="tpu_custom_call" | custom-call | tf_op jit(solution)/shard_map/pallas_call | solution.py:398
  52.1 2.0 %shard_map.65 = bf16[2048,1024]{1,0:T(8,128)(2,1)} custom-call(bf16[1920,1024]{1,0:T(8,128)(2,1)S(1)} %get-tuple-element.11.done, bf16[3,128,256]{2,1,0:T(8,128)(2,1)S(1)} %get-tuple-element.12.last, bf16[128,256]{1,0:T(8,128)(2,1)S(1)} %get-tuple-element.13.own_last, bf16[1024,1024]{1,0:T(8,128)(2,1)S(1)} %get-tuple-element.14.wall, ...), custom_call_target="tpu_custom_call" | custom-call | tf_op jit(solution)/shard_map/pallas_call | solution.py:434

commit v5 on v4

--- a/solution.py
+++ b/solution.py
@@ -57,7 +57,7 @@
     out, last, own_last, wall, par, gb,
     vals, raw, subs, owns, tstat, totals, tots,
     send_y, buf_y, send_z, buf_z, back_z, got_z, back_y, got_y, tile_stat, peer_stat, lhs,
-    load_sem, slot_sem, own_sem, sent, tot_sent, gb_sent, w_sent,
+    load_sem, slot_sem, own_sem, sent, tot_sent, w_sent,
     x_recv, wx_recv, wz_recv, wy_recv, wc_recv, gb_recv, st_recv, line_recv, near, lines, far,
 ):
     shuf, x = lax.axis_index("shuf"), lax.axis_index("rep")
@@ -128,8 +128,8 @@
 
     for d in range(1, NX):
         at = NX - d
-        send(gain, gb.at[at, 0], gb_sent, gb_recv, x_peer(d))
-        send(bias, gb.at[at, 1], gb_sent, gb_recv, x_peer(d))
+        send(gain, gb.at[at, 0], tot_sent, gb_recv, x_peer(d))
+        send(bias, gb.at[at, 1], tot_sent, gb_recv, x_peer(d))
 
     @pl.when(gathers)
     def _():
@@ -160,9 +160,9 @@
     def _():
         pl.semaphore_wait(barrier, NQ - 1 + NZ - 1)
         for d in range(1, NQ):
-            signal(lines.at[0], q_peer(d))
+            signal(lines, q_peer(d))
         for d in range(1, NZ):
-            signal(lines.at[1], z_peer(d))
+            signal(lines, z_peer(d))
 
     wait_for(vals, load_sem)
 
@@ -219,24 +219,21 @@
     r0, r1 = iota((SLOTS, SLOTS), 0), iota((SLOTS, SLOTS), 1)
     swap = jnp.where(r1 == ((r0 >> 1) & 7) * 16 + (r0 >> 4) * 2 + (r0 & 1), 1.0, 0.0).astype(BF16)
 
-    def line_known(i, peers):
-        @pl.when(is_head)
-        def _():
-            pl.semaphore_wait(lines.at[i], peers)
-            for d in range(1, NX):
-                signal(far.at[i], x_peer(d))
-
-        @pl.when(x != HEAD)
-        def _():
-            pl.semaphore_wait(far.at[i], 1)
-
-    line_known(0, NQ - 1)
+    @pl.when(is_head)
+    def _():
+        pl.semaphore_wait(lines, NQ - 1 + NZ - 1)
+        for d in range(1, NX):
+            signal(far, x_peer(d))
+
+    @pl.when(x != HEAD)
+    def _():
+        pl.semaphore_wait(far, 1)
+
     for d in range(1, NQ):
         p = lax.rem(q + d, NQ)
         send(totals.at[0], tot_y.at[q], tot_sent, line_recv.at[0], q_peer(d))
         send(send_y.at[p], buf_y.at[q], sent, line_recv.at[1], q_peer(d))
 
-    line_known(1, NZ - 1)
     wx_all = wall.at[pl.ds(0, (NX - 1) * 32), pl.ds(0, 256)]
     wz_all = wall.at[pl.ds(0, (NX - 1) * (NZ - 1) * 32), pl.ds(0, 256)]
     wy_all = wall.at[pl.ds(0, (NX - 1) * COLS), pl.ds(0, 768)]
@@ -362,8 +359,7 @@
     arrived_piece(EARLY + 2)
 
     wait_for(vals.at[pl.ds(0, SENT_BYTES // (2 * COLS))], sent)
-    wait_for(tots.at[pl.ds(0, NQ + NZ - 2)], tot_sent)
-    wait_for(gb.at[pl.ds(0, NX - 1)], gb_sent)
+    wait_for(tots.at[pl.ds(0, NQ + NZ - 2 + NX - 1)], tot_sent)
 
     @pl.when(gathers)
     def _():
@@ -407,7 +403,7 @@
             pltpu.SMEM((TILES,), jnp.int32),
             vmem((TILES, 2 * COLS), F32),
             vmem((2, 1, 2 * COLS), F32),
-            vmem((NQ + NZ, 1, 2 * COLS), F32),
+            vmem((NQ + NZ + 1, 1, 2 * COLS), F32),
             vmem((NQ, 16, MSG), BF16),
             vmem((NQ, 16, MSG), BF16),
             vmem((NZ, 16, MSG), BF16),
@@ -419,10 +415,10 @@
             vmem((TILES, 2 * COLS), BF16),
             vmem((NX - 1, 16, 2 * COLS), BF16),
             vmem((GROWS, NX * COLS), BF16),
-            dma, dma((2,)), dma, dma, dma, dma, dma,
+            dma, dma((2,)), dma, dma, dma, dma,
             dma((len(PIECES) - EARLY + 1,)), dma, dma, dma, dma, dma, dma, dma((6,)),
             pltpu.SemaphoreType.REGULAR,
-            pltpu.SemaphoreType.REGULAR((2,)), pltpu.SemaphoreType.REGULAR((2,)),
+            pltpu.SemaphoreType.REGULAR, pltpu.SemaphoreType.REGULAR,
         ],
         compiler_params=pltpu.CompilerParams(
             collective_id=0, has_side_effects=True, vmem_limit_bytes=32 * 1024 * 1024

time: 54.2 us -> 55.1 us (1.017)
  Pallas kernels: 54.1 us -> 55 us
    pallas_call x1, Pallas kernels: 52.1 us -> 53 us  [on_device(): pl.pallas_call(exchange, out_shape=results, in_specs=[hbm] * 6, out_specs...]
where the time goes in v5:
time: 55.1 us; the launch traced here: 55 us
  Pallas kernels  55 us (100%)
    pallas_call x1, Pallas kernels, on_device(): pl.pallas_call(exchange, out_shape=results, in_specs=[hbm] * 6, out_specs...  53 us
    pallas_call x1, Pallas kernels, on_device(): pl.pallas_call(finish, out_shape=jax.ShapeDtypeStruct((OROWS, OUT), BF16)...  2.02 us

profile of v5, /device:TPU:1, one launch (start us, length us, event | category | flops | bytes accessed | tf_op | source)
XLA Modules:
  0.0 55.0 jit_solution(6983757386920681442)
XLA Ops:
  0.0 53.0 %shard_map.64 = (bf16[1920,1024]{1,0:T(8,128)(2,1)S(1)}, bf16[3,128,256]{2,1,0:T(8,128)(2,1)S(1)}, bf16[128,256]{1,0:T(8,128)(2,1)S(1)}, bf16[1024,1024]{1,0:T(8...) custom-call(bf16[8192,256]{1,0:T(8,128)(2,1)} %values.1, s32[64]{0:T(128)} %subgroup.1, s32[64]{0:T(128)} %bitcast.1, ...), custom_call_target="tpu_custom_call" | custom-call | tf_op jit(solution)/shard_map/pallas_call | solution.py:394
  53.0 2.0 %shard_map.65 = bf16[2048,1024]{1,0:T(8,128)(2,1)} custom-call(bf16[1920,1024]{1,0:T(8,128)(2,1)S(1)} %get-tuple-element.11.done, bf16[3,128,256]{2,1,0:T(8,128)(2,1)S(1)} %get-tuple-element.12.last, bf16[128,256]{1,0:T(8,128)(2,1)S(1)} %get-tuple-element.13.own_last, bf16[1024,1024]{1,0:T(8,128)(2,1)S(1)} %get-tuple-element.14.wall, ...), custom_call_target="tpu_custom_call" | custom-call | tf_op jit(solution)/shard_map/pallas_call | solution.py:430
